TPU v7x, 32 devices: a whole 2x2x4 slice. The times are simulated.
32 devices in a mesh: rep: 4 (over x, core), mx: 2 (over y), my: 4 (over z).
Axes of the slice: x: 2, y: 2, z: 4, core: 2. Of those that a mesh axis runs over, the one named last changes fastest.
Arguments:
- coefficients: bfloat16 [2, 384, 384, 384], P(None, 'mx', 'my'), may hold values from -7.5 to 7.5
- noise_field: bfloat16 [128, 2, 1536, 1536], P(('rep', 'mx'), None, 'my'), may hold values from -96 to 96
- mode_table: bfloat16 [384, 1536], replicated, may hold values from -0.3125 to 0.3125
Outputs:
- update: bfloat16 [2, 384, 384, 384], P(None, 'mx', 'my', 'rep')
All inputs are finite; a program needn't handle non-finite values.
Results may differ from a plain program's by a relative error of at most 0.008.
Values may be sent and summed in bfloat16 or wider, within the bound.
A program may use at most 384 MiB of HBM per device.

v0:
```python
import jax
import jax.numpy as jnp
from jax import lax
from jax.sharding import PartitionSpec as P

DAMPING = 0.25


def body(coefficients, noise_field, mode_table):
    rep_index = lax.axis_index("rep")
    col_index = lax.axis_index("my")
    rep_count = lax.axis_size("rep")
    row_count = lax.axis_size("mx")
    col_count = lax.axis_size("my")
    planes_dev = noise_field.shape[0]
    planes_rep = planes_dev * row_count
    planes_all = planes_rep * rep_count
    mode_count = mode_table.shape[0]
    point_count = mode_table.shape[1]
    slab_first = point_count // 2 - planes_all // 2
    row_block = mode_count // row_count
    col_block = mode_count // col_count
    point_block = point_count // col_count
    own_block = mode_count // rep_count
    slab_own = lax.dynamic_slice_in_dim(
        mode_table, slab_first + rep_index * planes_rep, planes_rep, 1
    )
    zmodes = jnp.einsum(
        "pabk,kz->zpba", coefficients, slab_own, preferred_element_type=jnp.float32
    ).astype(jnp.bfloat16)
    zmodes = zmodes.reshape(planes_rep, 2, col_block * row_block)
    spread = lax.all_to_all(zmodes, "mx", split_axis=0, concat_axis=2, tiled=True)
    grouped = spread.reshape(planes_dev, 2, row_count, col_block, row_block)
    tiled_table = mode_table.reshape(row_count, row_block, point_count)
    own_points = lax.dynamic_slice_in_dim(tiled_table, col_index * point_block, point_block, 2)
    block_part = jnp.einsum(
        "zpsal,slx->zpax",
        lax.all_gather(grouped, "my", axis=3, tiled=True),
        own_points,
        preferred_element_type=jnp.float32,
    ).astype(jnp.bfloat16)
    wave_field = jnp.einsum(
        "zpax,ay->zpxy", block_part, mode_table, preferred_element_type=jnp.float32
    )
    wave_real = wave_field[:, 0]
    wave_imag = wave_field[:, 1]
    density = wave_real * wave_real + wave_imag * wave_imag
    noise_wide = noise_field.astype(jnp.float32)
    drive_term = jnp.stack(
        [
            density * (wave_imag - DAMPING * wave_real) + noise_wide[:, 0],
            density * (-wave_real - DAMPING * wave_imag) + noise_wide[:, 1],
        ],
        1,
    ).astype(jnp.bfloat16)
    proj_columns = jnp.einsum(
        "zpxy,ny->zpnx", drive_term, mode_table, preferred_element_type=jnp.float32
    ).astype(jnp.bfloat16)
    block_part = lax.all_to_all(proj_columns, "my", split_axis=2, concat_axis=3, tiled=True)
    folded = jnp.einsum(
        "zpax,slx->zpsal", block_part, tiled_table, preferred_element_type=jnp.float32
    ).astype(jnp.bfloat16)
    proj_rows = folded.reshape(
        block_part.shape[0], block_part.shape[1], row_count * col_block * row_block
    )
    gathered_rows = lax.all_to_all(proj_rows, "mx", split_axis=2, concat_axis=0, tiled=True)
    slab_back = lax.dynamic_slice_in_dim(mode_table, rep_index * own_block, own_block, 0)[
        :, slab_first : slab_first + planes_all
    ]
    portion = lax.all_gather(gathered_rows, "rep", axis=0, tiled=True)
    plane_grid = portion.reshape(portion.shape[0], 2, col_block, row_block)
    summed = jnp.einsum("zpba,nz->pabn", plane_grid, slab_back, preferred_element_type=jnp.float32)
    return summed.astype(jnp.bfloat16)


def solution(mesh):
    in_specs = (P(None, "mx", "my", None), P(("rep", "mx"), None, "my", None), P())
    out_specs = P(None, "mx", "my", "rep")
    return jax.shard_map(body, mesh=mesh, in_specs=in_specs, out_specs=out_specs, check_vma=False)
```

profile of v0, /device:TPU:0, one launch (start us, length us, event | category | flops | bytes accessed | tf_op | source)
XLA Modules:
  0.0 974.2 jit_solution(4171945368356783076)
XLA Ops:
  6.5 0.0 copy-start
  6.5 0.0 all-gather.3.cloned.1.call-start
  6.5 1.3 copy-done
  7.8 25.5 %convert_bitcast_fusion.3 = bf16[32,2,96,192]{2,0,3,1:T(8,128)(2,1)} fusion(bf16[2,192,96,384]{3,2,1,0:T(8,128)(2,1)} %param.3, bf16[384,1536]{1,0:T(8,128)(2,1)S(1)} %copy-done, s32[]{:T(128)S(6)} %select_n.10), kind=kOutput, calls=%fused_computation.17 | convolution fusion | flops 907149312 | bytes 30769156 | tf_op jit(solution)/shard_map/pabk,kz->zpba/dot_general | solution.py:28
  33.3 5.1 copy.45
  38.5 6.9 reshape.28
  45.3 31.8 %all_to_all.51 = bf16[32,2,18432]{2,1,0:T(2,128)(2,1)S(1)} all-to-all(bf16[32,2,18432]{2,1,0:T(2,128)(2,1)S(1)} %reshape.28), channel_id=1, replica_groups=mesh['rep'=4,'mx'=2,'my'=4] {'mx'}, dimensions={0} | all-to-all | bytes 4718592 | tf_op jit(solution)/shard_map/all_to_all | solution.py:32
  77.1 2.4 copy.52
  79.5 4.5 reshape.17
  84.0 0.0 all-gather.3.cloned.1.call-update
  84.0 0.2 all-gather.5.cloned.1.call-start
  84.2 37.8 %convert_element_type.34 = f32[16,2,384,1536]{3,2,1,0:T(8,128)} convert(bf16[16,2,384,1536]{3,2,1,0:T(8,128)(2,1)} %param.4) | non-fusion elementwise | flops 18874368 | bytes 113246208 | tf_op jit(solution)/shard_map/convert_element_type | solution.py:48
  122.1 180.8 %all-gather.3.cloned.1.call-done = bf16[16,2,2,384,192]{4,3,2,1,0:T(8,128)(2,1)} async-done(((bf16[16,2,2,96,192]{4,3,2,1,0:T(8,128)(2,1)}), bf16[16,2,2,384,192]{4,3,2,1,0:T(8,128)(2,1)}) %all-gather.3.cloned.1.call-update) | async-done | bytes 9437200 | tf_op jit(solution)/shard_map/all_gather | solution.py:38
  302.9 36.1 %fusion.6 = f32[16,2,384,1536]{3,2,1,0:T(8,128)} fusion(bf16[16,2,2,384,192]{4,3,2,1,0:T(8,128)(2,1)} %all-gather.3.cloned.1.call-done, bf16[384,1536]{1,0:T(8,128)(2,1)S(1)} %copy-done, bf16[2,192,1536]{2,1,0:T(8,128)(2,1)S(1)} %bitcast.69, s32[]{:T(128)S(6)} %select_n.11), kind=kOutput, calls=%fused_computation.10 | convolution fusion | flops 18124111872 | bytes 86409216 | tf_op jit(solution)/shard_map/zpax,ay->zpxy/dot_general | solution.py:42
  339.0 61.5 %fusion.1 = (bf16[16,1,384,1536]{3,2,1,0:T(8,128)(2,1)}, bf16[16,1,384,1536]{3,2,1,0:T(8,128)(2,1)}) fusion(f32[16,2,384,1536]{3,2,1,0:T(8,128)} %convert_element_type.34, f32[16,2,384,1536]{3,2,1,0:T(8,128)} %fusion.6), kind=kLoop, calls=%fused_computation.3 | loop fusion | flops 132120576 | bytes 188743680 | tf_op jit(solution)/shard_map/convert
  400.5 26.7 %convert_bitcast_fusion.1 = bf16[16,2,384,384]{2,3,1,0:T(8,128)(2,1)} fusion(bf16[16,1,384,1536]{3,2,1,0:T(8,128)(2,1)} %get-tuple-element.6, bf16[16,1,384,1536]{3,2,1,0:T(8,128)(2,1)} %get-tuple-element.5, bf16[384,1536]{1,0:T(8,128)(2,1)S(1)} %copy-done), kind=kOutput, calls=%fused_computation.15 | convolution fusion | flops 14519107584 | bytes 48365568 | tf_op jit(solution)/shard_map/zpxy,ny->zpnx/dot_general | solution.py:56
  427.2 23.9 %copy.29 = bf16[16,2,384,384]{3,1,0,2:T(2,128)(2,1)} copy(bf16[16,2,384,384]{2,3,1,0:T(8,128)(2,1)} %convert_bitcast_fusion.1) | data formatting | bytes 18874368 | tf_op jit(solution)/shard_map/convert_element_type | solution.py:58
  451.1 214.1 %all_to_all.52 = bf16[16,2,384,384]{3,1,0,2:T(2,128)(2,1)} all-to-all(bf16[16,2,384,384]{3,1,0,2:T(2,128)(2,1)} %copy.29), channel_id=1, replica_groups=mesh['rep'=4,'mx'=2,'my'=4] {'my'}, dimensions={2} | all-to-all | bytes 18874368 | tf_op jit(solution)/shard_map/all_to_all | solution.py:59
  665.3 10.9 %copy.30 = bf16[16,2,384,384]{3,2,1,0:T(8,128)(2,1)} copy(bf16[16,2,384,384]{3,1,0,2:T(2,128)(2,1)} %all_to_all.52) | data formatting | bytes 18874368 | tf_op jit(solution)/shard_map/all_to_all | solution.py:59
  676.2 10.6 %copy.31 = bf16[16,2,96,4,384]{4,3,2,1,0:T(4,128)(2,1)} copy(bf16[16,2,96,4,384]{4,2,3,1,0:T(8,128)(2,1)} %bitcast.73) | data formatting | bytes 18874368 | tf_op jit(solution)/shard_map/all_to_all | solution.py:59
  686.8 15.9 %reshape.25 = bf16[16,2,96,1536,1]{3,2,1,0,4:T(8,128)(2,1)} reshape(bf16[16,2,96,4,384]{4,3,2,1,0:T(4,128)(2,1)} %copy.31) | data formatting | bytes 18874368 | tf_op jit(solution)/shard_map/all_to_all | solution.py:59
  702.7 10.2 %convert_bitcast_fusion.2 = bf16[16,2,2,96,192]{4,3,2,1,0:T(8,128)(2,1)} fusion(bf16[2,192,1536,1,1]{2,1,0,4,3:T(8,128)(2,1)S(1)} %bitcast.68, bf16[16,2,96,1536,1]{3,2,1,0,4:T(8,128)(2,1)} %reshape.25), kind=kOutput, calls=%fused_computation.16 | convolution fusion | flops 3625058304 | bytes 12976128 | tf_op jit(solution)/shard_map/zpax,slx->zpsal/dot_general | solution.py:60
  712.8 35.2 %copy.46 = bf16[16,2,2,96,192]{0,1,4,3,2:T(2,128)(2,1)} copy(bf16[16,2,2,96,192]{4,3,2,1,0:T(8,128)(2,1)} %convert_bitcast_fusion.2) | data formatting | bytes 4718592 | tf_op jit(solution)/shard_map/reshape | solution.py:63
  748.1 27.3 %reshape.30 = bf16[2,2,294912]{2,1,0:T(2,128)(2,1)S(1)} reshape(bf16[36864,2,16]{2,1,0:T(2,128)(2,1)} %bitcast.70) | data formatting | bytes 4718592
  775.3 30.9 %all_to_all.53 = bf16[2,2,294912]{2,1,0:T(2,128)(2,1)} all-to-all(bf16[2,2,294912]{2,1,0:T(2,128)(2,1)S(1)} %reshape.30), channel_id=1, replica_groups=mesh['rep'=4,'mx'=2,'my'=4] {'mx'}, dimensions={0} | all-to-all | bytes 4718592 | tf_op jit(solution)/shard_map/all_to_all | solution.py:66
  806.2 22.4 %reshape.31 = bf16[36864,2,16]{2,1,0:T(2,128)(2,1)} reshape(bf16[2,2,294912]{2,1,0:T(2,128)(2,1)} %all_to_all.53) | data formatting | bytes 4718592
  828.6 35.6 %copy.34 = bf16[2,16,2,18432]{3,1,0,2:T(8,128)(2,1)} copy(bf16[2,16,2,18432]{1,2,3,0:T(2,128)(2,1)} %bitcast.71) | data formatting | bytes 4718592 | tf_op jit(solution)/shard_map/all_to_all | solution.py:66
  864.2 0.0 all-gather.5.cloned.1.call-update
  864.2 62.8 %all-gather.5.cloned.1.call-done = bf16[128,2,18432]{2,0,1:T(8,128)(2,1)} async-done(((bf16[32,2,18432]{2,0,1:T(8,128)(2,1)}), bf16[128,2,18432]{2,0,1:T(8,128)(2,1)}) %all-gather.5.cloned.1.call-update) | async-done | bytes 9437200 | tf_op jit(solution)/shard_map/all_gather | solution.py:70
  927.0 12.6 %copy.35 = bf16[128,2,18432]{0,2,1:T(8,128)(2,1)} copy(bf16[128,2,18432]{2,0,1:T(8,128)(2,1)} %all-gather.5.cloned.1.call-done) | data formatting | bytes 18874368 | tf_op jit(solution)/shard_map/all_gather | solution.py:70
  939.6 13.8 %convert_bitcast_fusion = bf16[2,192,96,96]{1,3,2,0:T(8,128)(2,1)} fusion(bf16[128,2,96,192]{0,3,2,1:T(8,128)(2,1)} %bitcast.72, bf16[384,1536]{1,0:T(8,128)(2,1)S(1)} %copy-done, s32[]{:T(128)S(6)} %select_n.9, s32[]{:T(128)S(6)} %add.30), kind=kOutput, calls=%fused_computation.14 | convolution fusion | flops 909508608 | bytes 16539656 | tf_op jit(solution)/shard_map/zpba,nz->pabn/dot_general | solution.py:72
  953.3 13.9 %copy.36 = bf16[2,192,96,96]{3,2,1,0:T(8,128)(2,1)} copy(bf16[2,192,96,96]{1,3,2,0:T(8,128)(2,1)} %convert_bitcast_fusion) | data formatting | bytes 14155776 | tf_op jit(solution)/shard_map/convert_element_type | solution.py:73
Async XLA Ops:
  6.5 1.3 copy-start
  6.5 296.3 %all-gather.3.cloned.1.call-start = ((), (), s32[]{:S(2)}) async-start(), calls=%async_computation.3 | async-start | bytes 15728640 | tf_op jit(solution)/shard_map/all_gather | solution.py:38
  84.0 843.0 %all-gather.5.cloned.1.call-start = ((), (), s32[]{:S(2)}) async-start(), calls=%async_computation.4 | async-start | bytes 11796480 | tf_op jit(solution)/shard_map/all_gather | solution.py:70
Sparse Core Ops, SparseCore 0:
  84.1 218.6 all-gather.2
  864.3 62.6 all-gather.4
where the time goes:
time: 986 us; the launch traced here: 974 us
  blocking collectives  277 us (28%)
  waiting for transfers between devices  244 us (25%)
  local copies, waits for them, and re-layouts  228 us (23%)
  matrix products  112 us (11%)
  other arithmetic  99.4 us (10%)
  between operations  13.6 us (1%)
    all_to_all x1, blocking collectives, body(): lax.all_to_all(proj_columns, 'my', split_axis=2, concat_axis=3, tiled=True)  214 us
    all_gather x1, waiting for transfers between devices, body(): lax.all_gather(grouped, 'my', axis=3, tiled=True)  181 us
    all_gather x1, waiting for transfers between devices, body(): portion = lax.all_gather(gathered_rows, 'rep', axis=0, tiled=True)  62.8 us
    another operation x1, other arithmetic  61.5 us
    unnamed x4, local copies, waits for them, and re-layouts  50.9 us
    convert_element_type x1, other arithmetic, body(): noise_wide = noise_field.astype(jnp.float32)  37.8 us
    all_to_all x3, local copies, waits for them, and re-layouts, body(): lax.all_to_all(proj_columns, 'my', split_axis=2, concat_axis=3, tiled=True)  37.4 us
    dot_general x1, matrix products, body(): jnp.einsum('zpax,ay->zpxy', block_part, mode_table, preferred_element_typ...  36.1 us
  transfers between devices with their start and end apart: 2, of which 2 were waited for; matrix products, arithmetic and copies ran while one was open for 4% of the time, Pallas kernels for 0%

commit v1 on v0

--- a/solution.py
+++ b/solution.py
@@ -4,6 +4,15 @@
 from jax.sharding import PartitionSpec as P
 
 DAMPING = 0.25
+
+
+def reach_indices_on_mesh(named_axis, mat):
+    return jnp.concatenate(
+        lax.all_to_all(
+            jnp.stack(jnp.split(mat, lax.psum(1, named_axis), axis=2)), named_axis, 0, 0
+        ),
+        axis=3,
+    )
 
 
 def body(coefficients, noise_field, mode_table):
@@ -56,7 +65,7 @@
     proj_columns = jnp.einsum(
         "zpxy,ny->zpnx", drive_term, mode_table, preferred_element_type=jnp.float32
     ).astype(jnp.bfloat16)
-    block_part = lax.all_to_all(proj_columns, "my", split_axis=2, concat_axis=3, tiled=True)
+    block_part = reach_indices_on_mesh("my", mat=proj_columns)
     folded = jnp.einsum(
         "zpax,slx->zpsal", block_part, tiled_table, preferred_element_type=jnp.float32
     ).astype(jnp.bfloat16)

time: 986 us -> 947 us (0.960)
  local copies, waits for them, and re-layouts: 228 us -> 201 us
    all_to_all x3 -> x0, local copies, waits for them, and re-layouts: 37.4 us -> none  [body(): lax.all_to_all(proj_columns, 'my', split_axis=2, concat_axis=3, tiled=True)]
    reshape x0 -> x2, local copies, waits for them, and re-layouts: none -> 32.2 us  [reach_indices_on_mesh(): jnp.concatenate(lax.all_to_all(jnp.stack(jnp.split(mat, lax.psum(1, named...]
    convert_element_type x1 -> x0, local copies, waits for them, and re-layouts: 23.9 us -> none  [body(): proj_columns = jnp.einsum('zpxy,ny->zpnx', drive_term, mode_table, prefer...]
    another operation x1 -> x2, other arithmetic: 61.5 us -> 62.9 us
where the time goes in v1:
time: 947 us; the launch traced here: 935 us
  blocking collectives  271 us (29%)
  waiting for transfers between devices  244 us (26%)
  local copies, waits for them, and re-layouts  201 us (21%)
  matrix products  105 us (11%)
  other arithmetic  101 us (11%)
  between operations  13.6 us (1%)
    all_to_all x1, blocking collectives, reach_indices_on_mesh(): lax.all_to_all(jnp.stack(jnp.split(mat, lax.psum(1, named_axis), axis=2))...  209 us
    all_gather x1, waiting for transfers between devices, body(): lax.all_gather(grouped, 'my', axis=3, tiled=True)  181 us
    all_gather x1, waiting for transfers between devices, body(): portion = lax.all_gather(gathered_rows, 'rep', axis=0, tiled=True)  62.8 us
    another operation x1, other arithmetic  61.4 us
    unnamed x4, local copies, waits for them, and re-layouts  50.9 us
    convert_element_type x1, other arithmetic, body(): noise_wide = noise_field.astype(jnp.float32)  37.8 us
    dot_general x1, matrix products, body(): jnp.einsum('zpax,ay->zpxy', block_part, mode_table, preferred_element_typ...  36.1 us
    all_to_all x1, local copies, waits for them, and re-layouts, body(): lax.all_to_all(proj_rows, 'mx', split_axis=2, concat_axis=0, tiled=True)  35.6 us
  transfers between devices with their start and end apart: 2, of which 2 were waited for; matrix products, arithmetic and copies ran while one was open for 4% of the time, Pallas kernels for 0%

profile of v1, /device:TPU:0, one launch (start us, length us, event | category | flops | bytes accessed | tf_op | source)
XLA Modules:
  0.0 935.4 jit_solution(10832351998650225365)
XLA Ops:
  6.5 0.0 copy-start
  6.5 0.0 all-gather.3.cloned.1.call-start
  6.5 1.3 copy-done
  7.8 25.5 %convert_bitcast_fusion.3 = bf16[32,2,96,192]{2,0,3,1:T(8,128)(2,1)} fusion(bf16[2,192,96,384]{3,2,1,0:T(8,128)(2,1)} %param.3, bf16[384,1536]{1,0:T(8,128)(2,1)S(1)} %copy-done, s32[]{:T(128)S(6)} %select_n.10), kind=kOutput, calls=%fused_computation.18 | convolution fusion | flops 907149312 | bytes 30769156 | tf_op jit(solution)/shard_map/pabk,kz->zpba/dot_general | solution.py:37
  33.3 5.1 copy.40
  38.5 6.9 reshape.36
  45.3 31.8 %all_to_all.38 = bf16[32,2,18432]{2,1,0:T(2,128)(2,1)S(1)} all-to-all(bf16[32,2,18432]{2,1,0:T(2,128)(2,1)S(1)} %reshape.36), channel_id=1, replica_groups=mesh['rep'=4,'mx'=2,'my'=4] {'mx'}, dimensions={0} | all-to-all | bytes 4718592 | tf_op jit(solution)/shard_map/all_to_all | solution.py:41
  77.1 2.4 copy.47
  79.5 4.5 reshape.23
  84.0 0.0 all-gather.3.cloned.1.call-update
  84.0 0.2 all-gather.5.cloned.1.call-start
  84.2 37.8 %convert_element_type.34 = f32[16,2,384,1536]{3,2,1,0:T(8,128)} convert(bf16[16,2,384,1536]{3,2,1,0:T(8,128)(2,1)} %param.4) | non-fusion elementwise | flops 18874368 | bytes 113246208 | tf_op jit(solution)/shard_map/convert_element_type | solution.py:57
  122.1 180.8 %all-gather.3.cloned.1.call-done = bf16[16,2,2,384,192]{4,3,2,1,0:T(8,128)(2,1)} async-done(((bf16[16,2,2,96,192]{4,3,2,1,0:T(8,128)(2,1)}), bf16[16,2,2,384,192]{4,3,2,1,0:T(8,128)(2,1)}) %all-gather.3.cloned.1.call-update) | async-done | bytes 9437200 | tf_op jit(solution)/shard_map/all_gather | solution.py:47
  302.9 36.1 %fusion.6 = f32[16,2,384,1536]{3,2,1,0:T(8,128)} fusion(bf16[16,2,2,384,192]{4,3,2,1,0:T(8,128)(2,1)} %all-gather.3.cloned.1.call-done, bf16[384,1536]{1,0:T(8,128)(2,1)S(1)} %copy-done, bf16[2,192,1536]{2,1,0:T(8,128)(2,1)S(1)} %bitcast.75, s32[]{:T(128)S(6)} %select_n.11), kind=kOutput, calls=%fused_computation.10 | convolution fusion | flops 18124111872 | bytes 86409216 | tf_op jit(solution)/shard_map/zpax,ay->zpxy/dot_general | solution.py:51
  339.0 61.4 %fusion.1 = (bf16[16,1,384,1536]{3,2,1,0:T(8,128)(2,1)}, bf16[16,1,384,1536]{3,2,1,0:T(8,128)(2,1)}) fusion(f32[16,2,384,1536]{3,2,1,0:T(8,128)} %convert_element_type.34, f32[16,2,384,1536]{3,2,1,0:T(8,128)} %fusion.6), kind=kLoop, calls=%fused_computation.3 | loop fusion | flops 132120576 | bytes 188743680 | tf_op jit(solution)/shard_map/convert
  400.4 19.5 %convert_bitcast_fusion.1 = bf16[16,2,384,384]{3,2,1,0:T(8,128)(2,1)S(1)} fusion(bf16[16,1,384,1536]{3,2,1,0:T(8,128)(2,1)} %get-tuple-element.6, bf16[16,1,384,1536]{3,2,1,0:T(8,128)(2,1)} %get-tuple-element.5, bf16[384,1536]{1,0:T(8,128)(2,1)S(1)} %copy-done), kind=kOutput, calls=%fused_computation.16 | convolution fusion | flops 14519107584 | bytes 48365568 | tf_op jit(solution)/shard_map/zpxy,ny->zpnx/dot_general | solution.py:65
  419.8 1.4 slice_bitcast_fusion.3
  421.3 1.5 pad_maximum_fusion
  422.8 208.7 %all_to_all.39 = bf16[4,16,2,96,384]{4,3,2,1,0:T(8,128)(2,1)S(1)} all-to-all(bf16[4,16,2,96,384]{4,3,2,1,0:T(8,128)(2,1)S(1)} %pad_maximum_fusion), channel_id=1, replica_groups=mesh['rep'=4,'mx'=2,'my'=4] {'my'}, dimensions={0} | all-to-all | bytes 18874368 | tf_op jit(solution)/shard_map/all_to_all | solution.py:11
  631.5 16.2 %copy.26 = bf16[16,2,96,4,384]{4,3,2,1,0:T(4,128)(2,1)} copy(bf16[16,2,96,4,384]{4,2,1,0,3:T(8,128)(2,1)S(1)} %bitcast.79) | data formatting | bytes 18874368 | tf_op jit(solution)/shard_map/reshape | solution.py:10
  647.8 15.9 %reshape.33 = bf16[16,2,96,1536,1]{3,2,1,0,4:T(8,128)(2,1)} reshape(bf16[16,2,96,4,384]{4,3,2,1,0:T(4,128)(2,1)} %copy.26) | data formatting | bytes 18874368 | tf_op jit(solution)/shard_map/reshape | solution.py:10
  663.7 10.1 %convert_bitcast_fusion.2 = bf16[16,2,2,96,192]{4,3,2,1,0:T(8,128)(2,1)} fusion(bf16[2,192,1536,1,1]{2,1,0,4,3:T(8,128)(2,1)S(1)} %bitcast.74, bf16[16,2,96,1536,1]{3,2,1,0,4:T(8,128)(2,1)} %reshape.33), kind=kOutput, calls=%fused_computation.17 | convolution fusion | flops 3625058304 | bytes 12976128 | tf_op jit(solution)/shard_map/zpax,slx->zpsal/dot_general | solution.py:69
  673.8 35.4 %copy.41 = bf16[16,2,2,96,192]{0,1,4,3,2:T(2,128)(2,1)} copy(bf16[16,2,2,96,192]{4,3,2,1,0:T(8,128)(2,1)} %convert_bitcast_fusion.2) | data formatting | bytes 4718592 | tf_op jit(solution)/shard_map/reshape | solution.py:72
  709.3 27.2 %reshape.38 = bf16[2,2,294912]{2,1,0:T(2,128)(2,1)S(1)} reshape(bf16[36864,2,16]{2,1,0:T(2,128)(2,1)} %bitcast.76) | data formatting | bytes 4718592
  736.5 30.9 %all_to_all.40 = bf16[2,2,294912]{2,1,0:T(2,128)(2,1)} all-to-all(bf16[2,2,294912]{2,1,0:T(2,128)(2,1)S(1)} %reshape.38), channel_id=1, replica_groups=mesh['rep'=4,'mx'=2,'my'=4] {'mx'}, dimensions={0} | all-to-all | bytes 4718592 | tf_op jit(solution)/shard_map/all_to_all | solution.py:75
  767.3 22.4 %reshape.39 = bf16[36864,2,16]{2,1,0:T(2,128)(2,1)} reshape(bf16[2,2,294912]{2,1,0:T(2,128)(2,1)} %all_to_all.40) | data formatting | bytes 4718592
  789.7 35.6 %copy.29 = bf16[2,16,2,18432]{3,1,0,2:T(8,128)(2,1)} copy(bf16[2,16,2,18432]{1,2,3,0:T(2,128)(2,1)} %bitcast.77) | data formatting | bytes 4718592 | tf_op jit(solution)/shard_map/all_to_all | solution.py:75
  825.3 0.0 all-gather.5.cloned.1.call-update
  825.3 62.8 %all-gather.5.cloned.1.call-done = bf16[128,2,18432]{2,0,1:T(8,128)(2,1)} async-done(((bf16[32,2,18432]{2,0,1:T(8,128)(2,1)}), bf16[128,2,18432]{2,0,1:T(8,128)(2,1)}) %all-gather.5.cloned.1.call-update) | async-done | bytes 9437200 | tf_op jit(solution)/shard_map/all_gather | solution.py:79
  888.1 12.6 %copy.30 = bf16[128,2,18432]{0,2,1:T(8,128)(2,1)} copy(bf16[128,2,18432]{2,0,1:T(8,128)(2,1)} %all-gather.5.cloned.1.call-done) | data formatting | bytes 18874368 | tf_op jit(solution)/shard_map/all_gather | solution.py:79
  900.7 13.8 %convert_bitcast_fusion = bf16[2,192,96,96]{1,3,2,0:T(8,128)(2,1)} fusion(bf16[128,2,96,192]{0,3,2,1:T(8,128)(2,1)} %bitcast.78, bf16[384,1536]{1,0:T(8,128)(2,1)S(1)} %copy-done, s32[]{:T(128)S(6)} %select_n.9, s32[]{:T(128)S(6)} %add.30), kind=kOutput, calls=%fused_computation.15 | convolution fusion | flops 909508608 | bytes 16539656 | tf_op jit(solution)/shard_map/zpba,nz->pabn/dot_general | solution.py:81
  914.5 13.9 %copy.31 = bf16[2,192,96,96]{3,2,1,0:T(8,128)(2,1)} copy(bf16[2,192,96,96]{1,3,2,0:T(8,128)(2,1)} %convert_bitcast_fusion) | data formatting | bytes 14155776 | tf_op jit(solution)/shard_map/convert_element_type | solution.py:82
Async XLA Ops:
  6.5 1.3 copy-start
  6.5 296.3 %all-gather.3.cloned.1.call-start = ((), (), s32[]{:S(2)}) async-start(), calls=%async_computation.3 | async-start | bytes 15728640 | tf_op jit(solution)/shard_map/all_gather | solution.py:47
  84.0 804.1 %all-gather.5.cloned.1.call-start = ((), (), s32[]{:S(2)}) async-start(), calls=%async_computation.4 | async-start | bytes 11796480 | tf_op jit(solution)/shard_map/all_gather | solution.py:79
Sparse Core Ops, SparseCore 0:
  84.1 218.6 all-gather.2
  825.5 62.6 all-gather.4
